TPU v7x, 256 devices: a whole 4x4x8 slice. The times are simulated.
256 devices in a mesh: track: 64 (over z, y_hi, x), lane: 4 (over y_lo, core).
Axes of the slice: x: 4, y: 4 (y_hi: 2, y_lo: 2; y = y_hi * 2 + y_lo), z: 8, core: 2. Of those that a mesh axis runs over, the one named last changes fastest.
Arguments:
- signal: float32 [64, 4, 4096, 512], P('track', 'lane'), may hold values from -8 to 8, as said below
- tap_gain: float32 [3, 512], replicated, may hold values from 0.3 to 1.2
Outputs:
- filtered: float32 [64, 4, 4096, 512], P('track', 'lane')
Inputs may be any that keep to these rules, and one draw needn't show every extreme that they name: signal holds numbers from -8 to 8.
All inputs are finite; a program needn't handle non-finite values.
Results may differ from a plain program's by a relative error of at most 0.0003.
Values sent between devices are 32-bit elements.
A program may use at most 64 MiB of HBM per device.

v0:
```python
import jax
import jax.numpy as jnp
from jax import lax
from jax.sharding import PartitionSpec as P


def passed_along(block, axis, distance):
    devices = range(lax.axis_size(axis))
    route = [((i - distance) % len(devices), i) for i in devices]
    return lax.ppermute(block, axis, route)


def local(signal, tap_gain):
    wide_in = signal.astype(jnp.float32)
    copy_1 = passed_along(signal, "track", 1)
    copy_2 = passed_along(signal, "track", 2)
    mixed = (
        tap_gain[0] * wide_in
        + tap_gain[1] * copy_1.astype(jnp.float32)
        + tap_gain[2] * copy_2.astype(jnp.float32)
    )
    filtered = jnp.tanh(mixed).astype(jnp.float32)
    return filtered


def solution(mesh):
    in_specs = (P("track", "lane", None, None), P())
    out_specs = P("track", "lane", None, None)
    return jax.shard_map(local, mesh=mesh, in_specs=in_specs, out_specs=out_specs, check_vma=False)
```

profile of v0, /device:TPU:1, one launch (start us, length us, event | category | flops | bytes accessed | tf_op | source)
XLA Modules:
  0.0 380.5 jit_solution(6127271403800749275)
XLA Ops:
  0.0 3.6 collective-permute-start.1
  3.6 0.3 collective-permute-start
  3.9 0.8 fusion
  4.7 187.9 %collective-permute-done.1 = f32[1,1,4096,512]{3,2,1,0:T(8,128)S(1)} collective-permute-done((f32[1,1,4096,512]{3,2,1,0:T(8,128)}, f32[1,1,4096,512]{3,2,1,0:T(8,128)S(1)}, u32[]{:S(2)}, u32[]{:S(2)}) %collective-permute-start.1) | collective-permute-done | bytes 8388640 | tf_op jit(solution)/shard_map/ppermute | solution.py:10
  192.6 181.0 %collective-permute-done = f32[1,1,4096,512]{3,2,1,0:T(8,128)S(1)} collective-permute-done((f32[1,1,4096,512]{3,2,1,0:T(8,128)}, f32[1,1,4096,512]{3,2,1,0:T(8,128)S(1)}, u32[]{:S(2)}, u32[]{:S(2)}) %collective-permute-start) | collective-permute-done | bytes 8388640 | tf_op jit(solution)/shard_map/ppermute | solution.py:10
  373.6 7.0 %add_tanh_fusion = f32[1,1,4096,512]{3,2,1,0:T(8,128)} fusion(f32[1,1,4096,512]{3,2,1,0:T(8,128)S(1)} %collective-permute-done.1, f32[1,1,4096,512]{3,2,1,0:T(8,128)S(1)} %collective-permute-done, f32[1,1,4096,512]{3,2,1,0:T(8,128)} %param.2, f32[512]{0:T(512)S(1)} %bitcast.4, f32[512]{0:T(512)S(1)} %bitcast.5, f32[512]{0:T(512)S(1)} %bitcast.3), kind=kLoop, calls=%fused_computation | loop fusion | flops 10485760 | bytes 33560576 | tf_op jit(solution)/shard_map/tanh | solution.py:22
Async XLA Ops:
  0.0 192.6 %collective-permute-start.1 = (f32[1,1,4096,512]{3,2,1,0:T(8,128)}, f32[1,1,4096,512]{3,2,1,0:T(8,128)S(1)}, u32[]{:S(2)}, u32[]{:S(2)}) collective-permute-start(f32[1,1,4096,512]{3,2,1,0:T(8,128)} %param.2), channel_id=1, source_target_pairs={{248,0},{252,4},{0,8},{4,12},{8,16},{12,20},{16,24},{20,28},{24,32... | collective-permute-start | bytes 25165832 | tf_op jit(solution)/shard_map/ppermute | solution.py:10
  3.6 370.0 %collective-permute-start = (f32[1,1,4096,512]{3,2,1,0:T(8,128)}, f32[1,1,4096,512]{3,2,1,0:T(8,128)S(1)}, u32[]{:S(2)}, u32[]{:S(2)}) collective-permute-start(f32[1,1,4096,512]{3,2,1,0:T(8,128)} %param.2), channel_id=1, source_target_pairs={{252,0},{0,4},{4,8},{8,12},{12,16},{16,20},{20,24},{24,28},{28,32}... | collective-permute-start | bytes 25165832 | tf_op jit(solution)/shard_map/ppermute | solution.py:10
where the time goes:
time: 381 us
  waiting for transfers between devices  369 us (97%)
  other arithmetic  6.95 us (2%)
  starting transfers between devices  3.88 us (1%)
    ppermute x2, waiting for transfers between devices, passed_along(): return lax.ppermute(block, axis, route)  369 us
  transfers between devices with their start and end apart: 2, of which 2 were waited for; matrix products, arithmetic and copies ran while one was open for 0% of the time, Pallas kernels for 0%

commit v1 on v0

v1 whole, which is shorter than its diff:
```python
import functools

import jax
import jax.numpy as jnp
from jax import lax
from jax.experimental import pallas as pl
from jax.experimental.pallas import tpu as pltpu
from jax.sharding import PartitionSpec as P

CHUNKS = 64
LAG = 4
LOADS = 4


def kernel(n, signal, gain, out, own, near, far, part, load_sem, near_send, near_recv, far_send, far_recv):
    steps = own.shape[0]
    rows = steps // CHUNKS
    t = lax.axis_index("track")
    x, y = t % 4, (t // 4) % 2
    odd = x % 2
    last = (x // 3) * y
    relay = (x // 2) * (1 - odd) * y
    first = odd * (1 - x // 3) * (1 - y)

    def piece(k):
        return pl.ds(pl.multiple_of(k * rows, rows), rows)

    def device(offset):
        return {"track": (t + offset + n) % n}

    def near_copy(src, k):
        return pltpu.make_async_remote_copy(
            src_ref=src.at[piece(k)],
            dst_ref=near.at[piece(k)],
            send_sem=near_send.at[k],
            recv_sem=near_recv.at[k],
            device_id=device(1),
            device_id_type=pl.DeviceIdType.MESH,
        )

    def far_copy(src, k, offset):
        return pltpu.make_async_remote_copy(
            src_ref=src.at[piece(k)],
            dst_ref=far.at[piece(k)],
            send_sem=far_send.at[k],
            recv_sem=far_recv.at[k],
            device_id=device(offset),
            device_id_type=pl.DeviceIdType.MESH,
        )

    loads = []
    for i in range(LOADS):
        block = pl.ds(i * (steps // LOADS), steps // LOADS)
        loads.append(pltpu.make_async_copy(signal.at[0, 0, block], own.at[block], load_sem.at[i]))
        loads[-1].start()

    barrier = pltpu.get_barrier_semaphore()

    def greet(offset):
        pl.semaphore_signal(barrier, inc=1, device_id=device(offset), device_id_type=pl.DeviceIdType.MESH)

    greet(-1)

    @pl.when(odd == 1)
    def _():
        greet(-2 - first)

    @pl.when(relay == 1)
    def _():
        greet(1)

    for load in loads:
        load.wait()
    pl.semaphore_wait(barrier, 1 + odd + relay)

    g0, g1, g2 = gain[0:1], gain[1:2], gain[2:3]

    @pl.when(odd == 1)
    def _():
        far_to = 2 - 3 * last

        def send(k, _):
            far_copy(own, k, far_to).start()
            return 0

        lax.fori_loop(0, CHUNKS, send, 0)

        def finish(k):
            far_copy(own, k, far_to).wait_recv()
            at = piece(k)
            out[at] = jnp.tanh(out[at] + g2 * far[at])

        def step(k, _):
            near_copy(part, k).wait_recv()
            at = piece(k)
            mine, before = own[at], near[at]
            part[at] = g1 * mine + g2 * before
            out[at] = g0 * mine + g1 * before
            near_copy(part, k).start()

            @pl.when(k >= LAG)
            def _():
                finish(k - LAG)

            return 0

        lax.fori_loop(0, CHUNKS, step, 0)

        def tail(k, _):
            finish(k)
            return 0

        lax.fori_loop(CHUNKS - LAG, CHUNKS, tail, 0)

        def drain(k, _):
            far_copy(own, k, far_to).wait_send()
            near_copy(part, k).wait_send()
            return 0

        lax.fori_loop(0, CHUNKS, drain, 0)

    @pl.when(odd == 0)
    def _():
        def send(k, _):
            near_copy(own, k).start()
            return 0

        lax.fori_loop(0, CHUNKS, send, 0)

        def step(k, _):
            @pl.when(relay == 1)
            def _():
                far_copy(far, k, 3).wait_recv()
                far_copy(far, k, 3).start()

            near_copy(own, k).wait_recv()
            at = piece(k)
            out[at] = jnp.tanh(g0 * own[at] + near[at])
            return 0

        lax.fori_loop(0, CHUNKS, step, 0)

        def drain(k, _):
            near_copy(own, k).wait_send()

            @pl.when(relay == 1)
            def _():
                far_copy(far, k, 3).wait_send()

            return 0

        lax.fori_loop(0, CHUNKS, drain, 0)


def local(n, signal, tap_gain):
    steps, channels = signal.shape[2:]
    whole = pltpu.VMEM((steps, channels), jnp.float32)
    sems = pltpu.SemaphoreType.DMA((CHUNKS,))
    out = pl.pallas_call(
        functools.partial(kernel, n),
        out_shape=pltpu.VMEM((steps, channels), jnp.float32),
        in_specs=[pl.BlockSpec(memory_space=pl.ANY), pl.BlockSpec(memory_space=pltpu.VMEM)],
        out_specs=pl.BlockSpec(memory_space=pltpu.VMEM),
        scratch_shapes=[whole] * 4 + [pltpu.SemaphoreType.DMA((LOADS,))] + [sems] * 4,
        compiler_params=pltpu.CompilerParams(
            collective_id=0, has_side_effects=True, vmem_limit_bytes=40 * 2**20
        ),
        name="echo",
    )(signal, tap_gain)
    return out.reshape(signal.shape)


def solution(mesh):
    in_specs = (P("track", "lane", None, None), P())
    out_specs = P("track", "lane", None, None)
    body = functools.partial(local, mesh.shape["track"])
    return jax.shard_map(body, mesh=mesh, in_specs=in_specs, out_specs=out_specs, check_vma=False)
```

time: 381 us -> 207 us (0.54)
  waiting for transfers between devices: 369 us -> 0 us
  Pallas kernels: 0 us -> 203 us
  other arithmetic: 6.95 us -> 0 us
  starting transfers between devices: 3.88 us -> 0 us
    ppermute x2 -> x0, waiting for transfers between devices: 369 us -> none  [passed_along(): return lax.ppermute(block, axis, route)]
    pallas_call x0 -> x1, Pallas kernels: none -> 203 us  [local(): pl.pallas_call(functools.partial(kernel, n), out_shape=pltpu.VMEM((steps,...]
    tanh x1 -> x0, other arithmetic: 6.95 us -> none  [local(): filtered = jnp.tanh(mixed).astype(jnp.float32)]
    unnamed x0 -> x3, local copies, waits for them, and re-layouts: none -> 4.1 us
    ppermute x2 -> x0, starting transfers between devices: 3.88 us -> none  [passed_along(): return lax.ppermute(block, axis, route)]
  transfers between devices with their start and end apart: 2 -> 0, of which waited for: 2 -> 0; matrix products, arithmetic and copies ran while one was open for 0% -> 0% of each run, Pallas kernels for 0% -> 0%
where the time goes in v1:
time: 207 us
  Pallas kernels  203 us (98%)
  local copies, waits for them, and re-layouts  4.1 us (2%)
    pallas_call x1, Pallas kernels, local(): pl.pallas_call(functools.partial(kernel, n), out_shape=pltpu.VMEM((steps,...  203 us

profile of v1, /device:TPU:1, one launch (start us, length us, event | category | flops | bytes accessed | tf_op | source)
XLA Modules:
  0.0 206.9 jit_solution(2844171331122437722)
XLA Ops:
  0.0 0.0 copy-start
  0.0 0.7 copy-done
  0.7 202.8 %echo.1 = f32[4096,512]{1,0:T(8,128)S(1)} custom-call(f32[1,1,4096,512]{3,2,1,0:T(8,128)} %signal.1, f32[3,512]{1,0:T(4,128)S(1)} %copy-done), custom_call_target="tpu_custom_call" | custom-call | tf_op jit(solution)/shard_map/echo/pallas_call | solution.py:159
  203.5 3.4 %copy.4 = f32[1,1,4096,512]{3,2,1,0:T(8,128)} copy(f32[1,1,4096,512]{3,2,1,0:T(8,128)S(1)} %bitcast.1) | data formatting | bytes 16777216
Async XLA Ops:
  0.0 0.7 copy-start

commit v2 on v0

v2 whole, which is shorter than its diff:
```python
import functools

import jax
import jax.numpy as jnp
from jax import lax
from jax.experimental import pallas as pl
from jax.experimental.pallas import tpu as pltpu
from jax.sharding import PartitionSpec as P

BLOCK = 64
SHARES = (16, 16, 16, 8, 4, 2, 2)


def kernel(n, sizes, signal, gain, out, own, near, far, part, gains, gain_sem, load_sem, near_send, near_recv, far_send, far_recv):
    half = own.shape[0] // 2
    count = len(sizes)
    starts = [sum(sizes[:i]) for i in range(count)]
    t = lax.axis_index("track")
    odd = t % 2
    raw_half = odd
    sum_half = 1 - odd
    far_to = 3 - 4 * odd
    far_from = 1 - 4 * odd

    def device(offset):
        return {"track": (t + offset + n) % n}

    barrier = pltpu.get_barrier_semaphore()
    for source in (-1, far_from):
        pl.semaphore_signal(barrier, inc=1, device_id=device(source), device_id_type=pl.DeviceIdType.MESH)

    def rows(side, i):
        return pl.ds(pl.multiple_of(side * half + starts[i], BLOCK), sizes[i])

    def near_copy(src, src_rows, side, i):
        return pltpu.make_async_remote_copy(
            src_ref=src.at[src_rows],
            dst_ref=near.at[rows(side, i)],
            send_sem=near_send.at[side * count + i],
            recv_sem=near_recv.at[side * count + i],
            device_id=device(1),
            device_id_type=pl.DeviceIdType.MESH,
        )

    def near_raw(i):
        return near_copy(own, rows(raw_half, i), raw_half, i)

    def near_sum(i):
        return near_copy(part, pl.ds(starts[i], sizes[i]), sum_half, i)

    def far_copy(src, side, i):
        return pltpu.make_async_remote_copy(
            src_ref=src.at[rows(side, i)],
            dst_ref=far.at[rows(side, i)],
            send_sem=far_send.at[side * count + i],
            recv_sem=far_recv.at[side * count + i],
            device_id=device(far_to),
            device_id_type=pl.DeviceIdType.MESH,
        )

    def load(side, i):
        at = rows(side, i)
        return pltpu.make_async_copy(signal.at[0, 0, at], own.at[at], load_sem.at[side * count + i])

    for i in range(count):
        load(raw_half, i).start()
        load(sum_half, i).start()
    gain_load = pltpu.make_async_copy(gain, gains, gain_sem)
    gain_load.start()
    gain_load.wait()
    pl.semaphore_wait(barrier, 2)

    for i in range(count):
        load(raw_half, i).wait()
        near_raw(i).start()
        load(sum_half, i).wait()
        far_copy(own, sum_half, i).start()

    g0, g1, g2 = gains[0:1], gains[1:2], gains[2:3]

    def blocks(side, i, body):
        def step(j, _):
            offset = starts[i] + j * BLOCK
            body(pl.ds(pl.multiple_of(side * half + offset, BLOCK), BLOCK), pl.ds(pl.multiple_of(offset, BLOCK), BLOCK))
            return 0

        lax.fori_loop(0, sizes[i] // BLOCK, step, 0)

    def add_up(at, inner):
        mine, before = own[at], near[at]
        part[inner] = g1 * mine + g2 * before
        out[at] = g0 * mine + g1 * before

    def finish_raw(at, _):
        out[at] = jnp.tanh(g0 * own[at] + near[at])

    def finish_sum(at, _):
        out[at] = jnp.tanh(out[at] + g2 * far[at])

    for i in range(count):
        near_sum(i).wait_recv()
        blocks(sum_half, i, add_up)
        far_copy(far, raw_half, i).wait_recv()
        far_copy(far, raw_half, i).start()
        near_sum(i).start()

    for i in range(count):
        near_raw(i).wait_recv()
        blocks(raw_half, i, finish_raw)
        far_copy(far, sum_half, i).wait_recv()
        blocks(sum_half, i, finish_sum)

    for i in range(count):
        near_raw(i).wait_send()
        near_sum(i).wait_send()
        far_copy(own, sum_half, i).wait_send()
        far_copy(far, raw_half, i).wait_send()


def local(n, signal, tap_gain):
    steps, channels = signal.shape[2:]
    sizes = [steps // 2 * share // sum(SHARES) for share in SHARES]

    def buffer(rows):
        return pltpu.VMEM((rows, channels), jnp.float32)

    sems = pltpu.SemaphoreType.DMA((2 * len(sizes),))
    out = pl.pallas_call(
        functools.partial(kernel, n, sizes),
        out_shape=buffer(steps),
        in_specs=[pl.BlockSpec(memory_space=pl.ANY)] * 2,
        out_specs=pl.BlockSpec(memory_space=pltpu.VMEM),
        scratch_shapes=[buffer(steps)] * 3
        + [buffer(steps // 2), buffer(tap_gain.shape[0]), pltpu.SemaphoreType.DMA]
        + [sems] * 5,
        compiler_params=pltpu.CompilerParams(
            collective_id=0, has_side_effects=True, vmem_limit_bytes=52 * 2**20
        ),
        name="echo",
    )(signal, tap_gain)
    return out.reshape(signal.shape)


def solution(mesh):
    in_specs = (P("track", "lane", None, None), P())
    out_specs = P("track", "lane", None, None)
    body = functools.partial(local, mesh.shape["track"])
    return jax.shard_map(body, mesh=mesh, in_specs=in_specs, out_specs=out_specs, check_vma=False)
```

time: 381 us -> 199 us (0.52)
  waiting for transfers between devices: 369 us -> 0 us
  Pallas kernels: 0 us -> 195 us
  other arithmetic: 6.95 us -> 0 us
  starting transfers between devices: 3.88 us -> 0 us
    ppermute x2 -> x0, waiting for transfers between devices: 369 us -> none  [passed_along(): return lax.ppermute(block, axis, route)]
    pallas_call x0 -> x1, Pallas kernels: none -> 195 us  [local(): pl.pallas_call(functools.partial(kernel, n, sizes), out_shape=buffer(step...]
    tanh x1 -> x0, other arithmetic: 6.95 us -> none  [local(): filtered = jnp.tanh(mixed).astype(jnp.float32)]
    ppermute x2 -> x0, starting transfers between devices: 3.88 us -> none  [passed_along(): return lax.ppermute(block, axis, route)]
  transfers between devices with their start and end apart: 2 -> 0, of which waited for: 2 -> 0; matrix products, arithmetic and copies ran while one was open for 0% -> 0% of each run, Pallas kernels for 0% -> 0%
where the time goes in v2:
time: 199 us
  Pallas kernels  195 us (98%)
  local copies, waits for them, and re-layouts  3.4 us (2%)
    pallas_call x1, Pallas kernels, local(): pl.pallas_call(functools.partial(kernel, n, sizes), out_shape=buffer(step...  195 us

profile of v2, /device:TPU:1, one launch (start us, length us, event | category | flops | bytes accessed | tf_op | source)
XLA Modules:
  0.0 198.7 jit_solution(8986396246526222011)
XLA Ops:
  0.0 195.3 %echo.1 = f32[4096,512]{1,0:T(8,128)S(1)} custom-call(f32[1,1,4096,512]{3,2,1,0:T(8,128)} %signal.1, f32[3,512]{1,0:T(4,128)} %gain.1), custom_call_target="tpu_custom_call" | custom-call | tf_op jit(solution)/shard_map/echo/pallas_call | solution.py:128
  195.3 3.4 %copy.4 = f32[1,1,4096,512]{3,2,1,0:T(8,128)} copy(f32[1,1,4096,512]{3,2,1,0:T(8,128)S(1)} %bitcast.1) | data formatting | bytes 16777216

commit v3 on v2

--- a/solution.py
+++ b/solution.py
@@ -8,10 +8,11 @@
 from jax.sharding import PartitionSpec as P
 
 BLOCK = 64
-SHARES = (16, 16, 16, 8, 4, 2, 2)
-
-
-def kernel(n, sizes, signal, gain, out, own, near, far, part, gains, gain_sem, load_sem, near_send, near_recv, far_send, far_recv):
+SHARES = (16, 16, 16, 8, 2, 2, 2, 2)
+DETOUR = 4
+
+
+def kernel(n, sizes, signal, gain, out, own, near, far, part, gains, gain_sem, load_sem, near_send, near_recv, far_send, far_recv, aside, aside_send, aside_recv):
     half = own.shape[0] // 2
     count = len(sizes)
     starts = [sum(sizes[:i]) for i in range(count)]
@@ -22,12 +23,19 @@
     far_to = 3 - 4 * odd
     far_from = 1 - 4 * odd
 
+    ending = t // (n - 2)
+    helper = (t // (n - 6)) * (1 - t // (n - 4))
+
     def device(offset):
         return {"track": (t + offset + n) % n}
 
     barrier = pltpu.get_barrier_semaphore()
     for source in (-1, far_from):
         pl.semaphore_signal(barrier, inc=1, device_id=device(source), device_id_type=pl.DeviceIdType.MESH)
+
+    @pl.when(helper == 1)
+    def _():
+        pl.semaphore_signal(barrier, inc=1, device_id=device(4), device_id_type=pl.DeviceIdType.MESH)
 
     def rows(side, i):
         return pl.ds(pl.multiple_of(side * half + starts[i], BLOCK), sizes[i])
@@ -58,6 +66,35 @@
             device_id_type=pl.DeviceIdType.MESH,
         )
 
+    def aside_copy(send_sem):
+        return pltpu.make_async_remote_copy(
+            src_ref=own.at[rows(1, DETOUR)],
+            dst_ref=aside,
+            send_sem=send_sem,
+            recv_sem=aside_recv,
+            device_id=device(-4),
+            device_id_type=pl.DeviceIdType.MESH,
+        )
+
+    def back_copy(dst, recv_sem, offset):
+        return pltpu.make_async_remote_copy(
+            src_ref=aside,
+            dst_ref=dst.at[rows(1, DETOUR)],
+            send_sem=aside_send,
+            recv_sem=recv_sem.at[count + DETOUR],
+            device_id=device(offset),
+            device_id_type=pl.DeviceIdType.MESH,
+        )
+
+    def start(copy, i, way):
+        if i != DETOUR:
+            copy.start()
+            return
+
+        @pl.when(way == 0)
+        def _():
+            copy.start()
+
     def load(side, i):
         at = rows(side, i)
         return pltpu.make_async_copy(signal.at[0, 0, at], own.at[at], load_sem.at[side * count + i])
@@ -67,15 +104,41 @@
         load(sum_half, i).start()
     gain_load = pltpu.make_async_copy(gain, gains, gain_sem)
     gain_load.start()
+    pl.semaphore_wait(barrier, 2 + ending)
+
+    for i in range(count):
+        if i == 0:
+            near_copy(signal.at[0, 0], rows(raw_half, i), raw_half, i).start()
+            far_copy(signal.at[0, 0], sum_half, i).start()
+            continue
+        load(raw_half, i).wait()
+        start(near_raw(i), i, ending * odd)
+        load(sum_half, i).wait()
+        start(far_copy(own, sum_half, i), i, ending * (1 - odd))
+
+    @pl.when(ending * odd == 1)
+    def _():
+        aside_copy(near_send.at[count + DETOUR]).start()
+
+    @pl.when(ending * (1 - odd) == 1)
+    def _():
+        aside_copy(far_send.at[count + DETOUR]).start()
+
+    @pl.when(helper == 1)
+    def _():
+        aside_copy(aside_send).wait_recv()
+
+    @pl.when(helper * odd == 1)
+    def _():
+        back_copy(near, near_recv, 5).start()
+
+    @pl.when(helper * (1 - odd) == 1)
+    def _():
+        back_copy(far, far_recv, 7).start()
+
     gain_load.wait()
-    pl.semaphore_wait(barrier, 2)
-
-    for i in range(count):
-        load(raw_half, i).wait()
-        near_raw(i).start()
-        load(sum_half, i).wait()
-        far_copy(own, sum_half, i).start()
-
+    load(raw_half, 0).wait()
+    load(sum_half, 0).wait()
     g0, g1, g2 = gains[0:1], gains[1:2], gains[2:3]
 
     def blocks(side, i, body):
@@ -115,6 +178,10 @@
         near_sum(i).wait_send()
         far_copy(own, sum_half, i).wait_send()
         far_copy(far, raw_half, i).wait_send()
+
+    @pl.when(helper == 1)
+    def _():
+        back_copy(far, far_recv, 7).wait_send()
 
 
 def local(n, signal, tap_gain):
@@ -132,7 +199,8 @@
         out_specs=pl.BlockSpec(memory_space=pltpu.VMEM),
         scratch_shapes=[buffer(steps)] * 3
         + [buffer(steps // 2), buffer(tap_gain.shape[0]), pltpu.SemaphoreType.DMA]
-        + [sems] * 5,
+        + [sems] * 5
+        + [buffer(sizes[DETOUR]), pltpu.SemaphoreType.DMA, pltpu.SemaphoreType.DMA],
         compiler_params=pltpu.CompilerParams(
             collective_id=0, has_side_effects=True, vmem_limit_bytes=52 * 2**20
         ),

time: 199 us -> 194 us (0.975)
  Pallas kernels: 195 us -> 190 us
    pallas_call x1, Pallas kernels: 195 us -> 190 us  [local(): pl.pallas_call(functools.partial(kernel, n, sizes), out_shape=buffer(step...]
where the time goes in v3:
time: 194 us; the launch traced here: 193 us
  Pallas kernels  190 us (98%)
  local copies, waits for them, and re-layouts  3.4 us (2%)
    pallas_call x1, Pallas kernels, local(): pl.pallas_call(functools.partial(kernel, n, sizes), out_shape=buffer(step...  190 us

profile of v3, /device:TPU:1, one launch (start us, length us, event | category | flops | bytes accessed | tf_op | source)
XLA Modules:
  0.0 193.3 jit_solution(12339655019666562013)
XLA Ops:
  0.0 189.9 %echo.1 = f32[4096,512]{1,0:T(8,128)S(1)} custom-call(f32[1,1,4096,512]{3,2,1,0:T(8,128)} %signal.1, f32[3,512]{1,0:T(4,128)} %gain.1), custom_call_target="tpu_custom_call" | custom-call | tf_op jit(solution)/shard_map/echo/pallas_call | solution.py:195
  189.9 3.4 %copy.4 = f32[1,1,4096,512]{3,2,1,0:T(8,128)} copy(f32[1,1,4096,512]{3,2,1,0:T(8,128)S(1)} %bitcast.1) | data formatting | bytes 16777216

commit v4 on v2

--- a/solution.py
+++ b/solution.py
@@ -7,11 +7,12 @@
 from jax.experimental.pallas import tpu as pltpu
 from jax.sharding import PartitionSpec as P
 
-BLOCK = 64
-SHARES = (16, 16, 16, 8, 4, 2, 2)
-
-
-def kernel(n, sizes, signal, gain, out, own, near, far, part, gains, gain_sem, load_sem, near_send, near_recv, far_send, far_recv):
+SHARES = (16, 24, 32, 32, 8, 2, 2, 6, 4, 2)
+LAG = 1
+DETOURS = (5, 6)
+
+
+def kernel(n, sizes, signal, gain, out, own, near, far, part, gains, gain_sem, load_sem, near_send, near_recv, far_send, far_recv, aside, aside_send, aside_recv, over, over_send, over_recv, via, via_send, via_recv):
     half = own.shape[0] // 2
     count = len(sizes)
     starts = [sum(sizes[:i]) for i in range(count)]
@@ -22,15 +23,41 @@
     far_to = 3 - 4 * odd
     far_from = 1 - 4 * odd
 
+    cross = t % 4 // 2
+    up = t // 4 % 2
+    ending = t // (n - 2)
+    helper = (t // (n - 6)) * (1 - t // (n - 4))
+    second = (t // (n - 8)) * (1 - t // (n - 6))
+
     def device(offset):
         return {"track": (t + offset + n) % n}
 
     barrier = pltpu.get_barrier_semaphore()
-    for source in (-1, far_from):
+
+    def greet(source):
         pl.semaphore_signal(barrier, inc=1, device_id=device(source), device_id_type=pl.DeviceIdType.MESH)
 
+    greet(-1)
+    greet(far_from)
+
+    @pl.when(cross == 1)
+    def _():
+        greet(-4)
+
+        @pl.when(up == 0)
+        def _():
+            greet(4)
+
+    @pl.when(cross == 0)
+    def _():
+        greet(3 - 2 * odd)
+
+    @pl.when(second == 1)
+    def _():
+        greet(3 - 2 * odd)
+
     def rows(side, i):
-        return pl.ds(pl.multiple_of(side * half + starts[i], BLOCK), sizes[i])
+        return pl.ds(pl.multiple_of(side * half + starts[i], 8), sizes[i])
 
     def near_copy(src, src_rows, side, i):
         return pltpu.make_async_remote_copy(
@@ -58,6 +85,106 @@
             device_id_type=pl.DeviceIdType.MESH,
         )
 
+    def inner(i):
+        return pl.ds(starts[i], sizes[i])
+
+    def over_copy(src, src_rows, send_sem, i, offset):
+        return pltpu.make_async_remote_copy(
+            src_ref=src.at[src_rows],
+            dst_ref=over.at[inner(i)],
+            send_sem=send_sem.at[i],
+            recv_sem=over_recv.at[i],
+            device_id=device(offset),
+            device_id_type=pl.DeviceIdType.MESH,
+        )
+
+    def via_copy(src, src_rows, send_sem, i):
+        return pltpu.make_async_remote_copy(
+            src_ref=src.at[src_rows],
+            dst_ref=via.at[inner(i)],
+            send_sem=send_sem.at[i],
+            recv_sem=via_recv.at[i],
+            device_id=device(-4),
+            device_id_type=pl.DeviceIdType.MESH,
+        )
+
+    def leave_row(src, src_rows, send_sem, i):
+        @pl.when(up == 0)
+        def _():
+            over_copy(src, src_rows, send_sem, i, 4).start()
+
+        @pl.when(up == 1)
+        def _():
+            via_copy(src, src_rows, send_sem, i).start()
+
+    def change_plane(i):
+        @pl.when(cross * (1 - up) == 1)
+        def _():
+            via_copy(via, inner(i), via_send, i).wait_recv()
+            over_copy(via, inner(i), via_send, i, 8).start()
+
+    def landing_copy(dst, recv_sem, i):
+        return pltpu.make_async_remote_copy(
+            src_ref=over.at[inner(i)],
+            dst_ref=dst.at[rows(0, i)],
+            send_sem=over_send.at[i],
+            recv_sem=recv_sem.at[i],
+            device_id=device(-1 - 2 * odd),
+            device_id_type=pl.DeviceIdType.MESH,
+        )
+
+    def land(i):
+        @pl.when(cross == 1)
+        def _():
+            over_copy(over, inner(i), over_send, i, 4).wait_recv()
+
+        @pl.when(cross * odd == 1)
+        def _():
+            landing_copy(near, near_recv, i).start()
+
+        @pl.when(cross * (1 - odd) == 1)
+        def _():
+            landing_copy(far, far_recv, i).start()
+
+    def parked(j):
+        return pl.ds(j * sizes[DETOURS[0]], sizes[DETOURS[j]])
+
+    def aside_copy(src, j, send_sem, offset):
+        return pltpu.make_async_remote_copy(
+            src_ref=src,
+            dst_ref=aside.at[parked(j)],
+            send_sem=send_sem,
+            recv_sem=aside_recv.at[j],
+            device_id=device(offset),
+            device_id_type=pl.DeviceIdType.MESH,
+        )
+
+    def back_copy(dst, recv_sem, j, offset):
+        return pltpu.make_async_remote_copy(
+            src_ref=aside.at[parked(j)],
+            dst_ref=dst.at[rows(1, DETOURS[j])],
+            send_sem=aside_send.at[j],
+            recv_sem=recv_sem.at[count + DETOURS[j]],
+            device_id=device(offset),
+            device_id_type=pl.DeviceIdType.MESH,
+        )
+
+    def onward_copy():
+        return aside_copy(aside.at[parked(1)], 1, aside_send.at[1], -1 - 2 * odd)
+
+    def leave_aside(send_sem):
+        for j, i in enumerate(DETOURS):
+            aside_copy(signal.at[0, 0, rows(1, i)], j, send_sem.at[count + i], -4).start()
+
+    def start(copy, i, way):
+        if i not in DETOURS:
+            copy.start()
+            return
+
+        @pl.when(way == 0)
+        def _():
+            copy.start()
+
     def load(side, i):
         at = rows(side, i)
         return pltpu.make_async_copy(signal.at[0, 0, at], own.at[at], load_sem.at[side * count + i])
@@ -67,24 +194,53 @@
         load(sum_half, i).start()
     gain_load = pltpu.make_async_copy(gain, gains, gain_sem)
     gain_load.start()
+    pl.semaphore_wait(barrier, 2 + cross * (2 + up) + helper)
+
+    near_copy(signal.at[0, 0], rows(raw_half, 0), raw_half, 0).start()
+    far_copy(signal.at[0, 0], sum_half, 0).start()
+
+    @pl.when(ending * odd == 1)
+    def _():
+        leave_aside(near_send)
+
+    @pl.when(ending * (1 - odd) == 1)
+    def _():
+        leave_aside(far_send)
+
+    @pl.when(helper == 1)
+    def _():
+        for j in range(2):
+            aside_copy(aside.at[parked(j)], j, aside_send.at[j], -4).wait_recv()
+        onward_copy().start()
+
+    @pl.when(helper * odd == 1)
+    def _():
+        back_copy(near, near_recv, 0, 5).start()
+
+    @pl.when(helper * (1 - odd) == 1)
+    def _():
+        back_copy(far, far_recv, 0, 7).start()
+
+    for i in range(1, count):
+        load(raw_half, i).wait()
+        start(near_raw(i), i, ending * odd)
+        load(sum_half, i).wait()
+        start(far_copy(own, sum_half, i), i, ending * (1 - odd))
+
     gain_load.wait()
-    pl.semaphore_wait(barrier, 2)
-
-    for i in range(count):
-        load(raw_half, i).wait()
-        near_raw(i).start()
-        load(sum_half, i).wait()
-        far_copy(own, sum_half, i).start()
-
+    load(raw_half, 0).wait()
+    load(sum_half, 0).wait()
     g0, g1, g2 = gains[0:1], gains[1:2], gains[2:3]
 
     def blocks(side, i, body):
+        block = 64 if sizes[i] % 64 == 0 else 16
+
         def step(j, _):
-            offset = starts[i] + j * BLOCK
-            body(pl.ds(pl.multiple_of(side * half + offset, BLOCK), BLOCK), pl.ds(pl.multiple_of(offset, BLOCK), BLOCK))
+            offset = starts[i] + j * block
+            body(pl.ds(pl.multiple_of(side * half + offset, 8), block), pl.ds(pl.multiple_of(offset, 8), block))
             return 0
 
-        lax.fori_loop(0, sizes[i] // BLOCK, step, 0)
+        lax.fori_loop(0, sizes[i] // block, step, 0)
 
     def add_up(at, inner):
         mine, before = own[at], near[at]
@@ -101,8 +257,45 @@
         near_sum(i).wait_recv()
         blocks(sum_half, i, add_up)
         far_copy(far, raw_half, i).wait_recv()
-        far_copy(far, raw_half, i).start()
-        near_sum(i).start()
+
+        @pl.when(cross * (1 - odd) == 0)
+        def _():
+            far_copy(far, raw_half, i).start()
+
+        @pl.when(cross * (1 - odd) == 1)
+        def _():
+            leave_row(far, rows(0, i), far_send, i)
+
+        @pl.when(cross * odd == 0)
+        def _():
+            near_sum(i).start()
+
+        @pl.when(cross * odd == 1)
+        def _():
+            leave_row(part, inner(i), near_send, i)
+
+        if i >= LAG:
+            change_plane(i - LAG)
+        if i >= 2 * LAG:
+            land(i - 2 * LAG)
+        if i == 1:
+
+            @pl.when(second == 1)
+            def _():
+                onward_copy().wait_recv()
+
+            @pl.when(second * (1 - odd) == 1)
+            def _():
+                back_copy(near, near_recv, 1, 8).start()
+
+            @pl.when(second * odd == 1)
+            def _():
+                back_copy(far, far_recv, 1, 8).start()
+
+    for i in range(count - LAG, count):
+        change_plane(i)
+    for i in range(count - 2 * LAG, count):
+        land(i)
 
     for i in range(count):
         near_raw(i).wait_recv()
@@ -116,6 +309,22 @@
         far_copy(own, sum_half, i).wait_send()
         far_copy(far, raw_half, i).wait_send()
 
+        @pl.when(cross == 1)
+        def _():
+            landing_copy(far, far_recv, i).wait_send()
+
+        @pl.when(cross * (1 - up) == 1)
+        def _():
+            over_copy(via, inner(i), via_send, i, 8).wait_send()
+
+    @pl.when(helper == 1)
+    def _():
+        back_copy(far, far_recv, 0, 7).wait_send()
+
+    @pl.when(helper + second == 1)
+    def _():
+        back_copy(far, far_recv, 1, 8).wait_send()
+
 
 def local(n, signal, tap_gain):
     steps, channels = signal.shape[2:]
@@ -124,6 +333,7 @@
     def buffer(rows):
         return pltpu.VMEM((rows, channels), jnp.float32)
 
+    few = pltpu.SemaphoreType.DMA((len(sizes),))
     sems = pltpu.SemaphoreType.DMA((2 * len(sizes),))
     out = pl.pallas_call(
         functools.partial(kernel, n, sizes),
@@ -132,7 +342,9 @@
         out_specs=pl.BlockSpec(memory_space=pltpu.VMEM),
         scratch_shapes=[buffer(steps)] * 3
         + [buffer(steps // 2), buffer(tap_gain.shape[0]), pltpu.SemaphoreType.DMA]
-        + [sems] * 5,
+        + [sems] * 5
+        + [buffer(2 * sizes[DETOURS[0]]), pltpu.SemaphoreType.DMA((2,)), pltpu.SemaphoreType.DMA((2,))]
+        + [buffer(steps // 2), few, few] * 2,
         compiler_params=pltpu.CompilerParams(
             collective_id=0, has_side_effects=True, vmem_limit_bytes=52 * 2**20
         ),

time: 199 us -> 193 us (0.970)
  Pallas kernels: 195 us -> 189 us
    pallas_call x1, Pallas kernels: 195 us -> 189 us  [local(): pl.pallas_call(functools.partial(kernel, n, sizes), out_shape=buffer(step...]
where the time goes in v4:
time: 193 us
  Pallas kernels  189 us (98%)
  local copies, waits for them, and re-layouts  3.4 us (2%)
    pallas_call x1, Pallas kernels, local(): pl.pallas_call(functools.partial(kernel, n, sizes), out_shape=buffer(step...  189 us

profile of v4, /device:TPU:1, one launch (start us, length us, event | category | flops | bytes accessed | tf_op | source)
XLA Modules:
  0.0 192.5 jit_solution(12554325753488803941)
XLA Ops:
  0.0 189.1 %echo.1 = f32[4096,512]{1,0:T(8,128)S(1)} custom-call(f32[1,1,4096,512]{3,2,1,0:T(8,128)} %signal.1, f32[3,512]{1,0:T(4,128)} %gain.1), custom_call_target="tpu_custom_call" | custom-call | tf_op jit(solution)/shard_map/echo/pallas_call | solution.py:338
  189.1 3.4 %copy.4 = f32[1,1,4096,512]{3,2,1,0:T(8,128)} copy(f32[1,1,4096,512]{3,2,1,0:T(8,128)S(1)} %bitcast.1) | data formatting | bytes 16777216

commit v5 on v4

--- a/solution.py
+++ b/solution.py
@@ -7,7 +7,7 @@
 from jax.experimental.pallas import tpu as pltpu
 from jax.sharding import PartitionSpec as P
 
-SHARES = (16, 24, 32, 32, 8, 2, 2, 6, 4, 2)
+SHARES = (8, 16, 28, 34, 22, 2, 1, 9, 5, 3)
 LAG = 1
 DETOURS = (5, 6)
 
@@ -63,7 +63,7 @@
         return pltpu.make_async_remote_copy(
             src_ref=src.at[src_rows],
             dst_ref=near.at[rows(side, i)],
-            send_sem=near_send.at[side * count + i],
+            send_sem=near_send,
             recv_sem=near_recv.at[side * count + i],
             device_id=device(1),
             device_id_type=pl.DeviceIdType.MESH,
@@ -79,7 +79,7 @@
         return pltpu.make_async_remote_copy(
             src_ref=src.at[rows(side, i)],
             dst_ref=far.at[rows(side, i)],
-            send_sem=far_send.at[side * count + i],
+            send_sem=far_send,
             recv_sem=far_recv.at[side * count + i],
             device_id=device(far_to),
             device_id_type=pl.DeviceIdType.MESH,
@@ -92,7 +92,7 @@
         return pltpu.make_async_remote_copy(
             src_ref=src.at[src_rows],
             dst_ref=over.at[inner(i)],
-            send_sem=send_sem.at[i],
+            send_sem=send_sem,
             recv_sem=over_recv.at[i],
             device_id=device(offset),
             device_id_type=pl.DeviceIdType.MESH,
@@ -102,7 +102,7 @@
         return pltpu.make_async_remote_copy(
             src_ref=src.at[src_rows],
             dst_ref=via.at[inner(i)],
-            send_sem=send_sem.at[i],
+            send_sem=send_sem,
             recv_sem=via_recv.at[i],
             device_id=device(-4),
             device_id_type=pl.DeviceIdType.MESH,
@@ -127,7 +127,7 @@
         return pltpu.make_async_remote_copy(
             src_ref=over.at[inner(i)],
             dst_ref=dst.at[rows(0, i)],
-            send_sem=over_send.at[i],
+            send_sem=over_send,
             recv_sem=recv_sem.at[i],
             device_id=device(-1 - 2 * odd),
             device_id_type=pl.DeviceIdType.MESH,
@@ -174,7 +174,7 @@
 
     def leave_aside(send_sem):
         for j, i in enumerate(DETOURS):
-            aside_copy(signal.at[0, 0, rows(1, i)], j, send_sem.at[count + i], -4).start()
+            aside_copy(signal.at[0, 0, rows(1, i)], j, send_sem, -4).start()
 
     def start(copy, i, way):
         if i not in DETOURS:
@@ -303,19 +303,26 @@
         far_copy(far, sum_half, i).wait_recv()
         blocks(sum_half, i, finish_sum)
 
-    for i in range(count):
-        near_raw(i).wait_send()
-        near_sum(i).wait_send()
-        far_copy(own, sum_half, i).wait_send()
-        far_copy(far, raw_half, i).wait_send()
-
-        @pl.when(cross == 1)
-        def _():
-            landing_copy(far, far_recv, i).wait_send()
-
-        @pl.when(cross * (1 - up) == 1)
-        def _():
-            over_copy(via, inner(i), via_send, i, 8).wait_send()
+    def sent(buffer, send_sem, recv_sem):
+        pltpu.make_async_remote_copy(
+            src_ref=buffer,
+            dst_ref=buffer,
+            send_sem=send_sem,
+            recv_sem=recv_sem.at[0],
+            device_id=device(1),
+            device_id_type=pl.DeviceIdType.MESH,
+        ).wait_send()
+
+    sent(near, near_send, near_recv)
+    sent(far, far_send, far_recv)
+
+    @pl.when(cross == 1)
+    def _():
+        sent(over, over_send, over_recv)
+
+    @pl.when(cross * (1 - up) == 1)
+    def _():
+        sent(via, via_send, via_recv)
 
     @pl.when(helper == 1)
     def _():
@@ -333,6 +340,7 @@
     def buffer(rows):
         return pltpu.VMEM((rows, channels), jnp.float32)
 
+    one = pltpu.SemaphoreType.DMA
     few = pltpu.SemaphoreType.DMA((len(sizes),))
     sems = pltpu.SemaphoreType.DMA((2 * len(sizes),))
     out = pl.pallas_call(
@@ -341,10 +349,10 @@
         in_specs=[pl.BlockSpec(memory_space=pl.ANY)] * 2,
         out_specs=pl.BlockSpec(memory_space=pltpu.VMEM),
         scratch_shapes=[buffer(steps)] * 3
-        + [buffer(steps // 2), buffer(tap_gain.shape[0]), pltpu.SemaphoreType.DMA]
-        + [sems] * 5
+        + [buffer(steps // 2), buffer(tap_gain.shape[0]), one]
+        + [sems, one, sems, one, sems]
         + [buffer(2 * sizes[DETOURS[0]]), pltpu.SemaphoreType.DMA((2,)), pltpu.SemaphoreType.DMA((2,))]
-        + [buffer(steps // 2), few, few] * 2,
+        + [buffer(steps // 2), one, few] * 2,
         compiler_params=pltpu.CompilerParams(
             collective_id=0, has_side_effects=True, vmem_limit_bytes=52 * 2**20
         ),

time: 193 us -> 192 us (level)
  no operation moved by 1% of the time
where the time goes in v5:
time: 192 us
  Pallas kernels  189 us (98%)
  local copies, waits for them, and re-layouts  3.4 us (2%)
    pallas_call x1, Pallas kernels, local(): pl.pallas_call(functools.partial(kernel, n, sizes), out_shape=buffer(step...  189 us

profile of v5, /device:TPU:1, one launch (start us, length us, event | category | flops | bytes accessed | tf_op | source)
XLA Modules:
  0.0 192.0 jit_solution(2093781233306431644)
XLA Ops:
  0.0 188.6 %echo.1 = f32[4096,512]{1,0:T(8,128)S(1)} custom-call(f32[1,1,4096,512]{3,2,1,0:T(8,128)} %signal.1, f32[3,512]{1,0:T(4,128)} %gain.1), custom_call_target="tpu_custom_call" | custom-call | tf_op jit(solution)/shard_map/echo/pallas_call | solution.py:346
  188.6 3.4 %copy.4 = f32[1,1,4096,512]{3,2,1,0:T(8,128)} copy(f32[1,1,4096,512]{3,2,1,0:T(8,128)S(1)} %bitcast.1) | data formatting | bytes 16777216

commit v6 on v5

--- a/solution.py
+++ b/solution.py
@@ -233,7 +233,7 @@
     g0, g1, g2 = gains[0:1], gains[1:2], gains[2:3]
 
     def blocks(side, i, body):
-        block = 64 if sizes[i] % 64 == 0 else 16
+        block = next(b for b in (64, 48, 32, 16) if sizes[i] % b == 0)
 
         def step(j, _):
             offset = starts[i] + j * block
@@ -297,11 +297,15 @@
     for i in range(count - 2 * LAG, count):
         land(i)
 
-    for i in range(count):
+    for i in range(count - 1):
         near_raw(i).wait_recv()
         blocks(raw_half, i, finish_raw)
         far_copy(far, sum_half, i).wait_recv()
         blocks(sum_half, i, finish_sum)
+    far_copy(far, sum_half, count - 1).wait_recv()
+    blocks(sum_half, count - 1, finish_sum)
+    near_raw(count - 1).wait_recv()
+    blocks(raw_half, count - 1, finish_raw)
 
     def sent(buffer, send_sem, recv_sem):
         pltpu.make_async_remote_copy(

time: 192 us -> 192 us (level)
  no operation moved by 1% of the time
where the time goes in v6:
time: 192 us
  Pallas kernels  189 us (98%)
  local copies, waits for them, and re-layouts  3.4 us (2%)
    pallas_call x1, Pallas kernels, local(): pl.pallas_call(functools.partial(kernel, n, sizes), out_shape=buffer(step...  189 us

profile of v6, /device:TPU:1, one launch (start us, length us, event | category | flops | bytes accessed | tf_op | source)
XLA Modules:
  0.0 191.9 jit_solution(15226243311468956947)
XLA Ops:
  0.0 188.5 %echo.1 = f32[4096,512]{1,0:T(8,128)S(1)} custom-call(f32[1,1,4096,512]{3,2,1,0:T(8,128)} %signal.1, f32[3,512]{1,0:T(4,128)} %gain.1), custom_call_target="tpu_custom_call" | custom-call | tf_op jit(solution)/shard_map/echo/pallas_call | solution.py:350
  188.5 3.4 %copy.4 = f32[1,1,4096,512]{3,2,1,0:T(8,128)} copy(f32[1,1,4096,512]{3,2,1,0:T(8,128)S(1)} %bitcast.1) | data formatting | bytes 16777216

commit v7 on v5

--- a/solution.py
+++ b/solution.py
@@ -7,7 +7,7 @@
 from jax.experimental.pallas import tpu as pltpu
 from jax.sharding import PartitionSpec as P
 
-SHARES = (8, 16, 28, 34, 22, 2, 1, 9, 5, 3)
+SHARES = (8, 16, 28, 34, 28, 2, 1, 8, 3)
 LAG = 1
 DETOURS = (5, 6)
 

time: 192 us -> 192 us (level)
  no operation moved by 1% of the time
where the time goes in v7:
time: 192 us
  Pallas kernels  189 us (98%)
  local copies, waits for them, and re-layouts  3.4 us (2%)
    pallas_call x1, Pallas kernels, local(): pl.pallas_call(functools.partial(kernel, n, sizes), out_shape=buffer(step...  189 us

profile of v7, /device:TPU:1, one launch (start us, length us, event | category | flops | bytes accessed | tf_op | source)
XLA Modules:
  0.0 191.9 jit_solution(5021216195383469820)
XLA Ops:
  0.0 188.5 %echo.1 = f32[4096,512]{1,0:T(8,128)S(1)} custom-call(f32[1,1,4096,512]{3,2,1,0:T(8,128)} %signal.1, f32[3,512]{1,0:T(4,128)} %gain.1), custom_call_target="tpu_custom_call" | custom-call | tf_op jit(solution)/shard_map/echo/pallas_call | solution.py:346
  188.5 3.4 %copy.4 = f32[1,1,4096,512]{3,2,1,0:T(8,128)} copy(f32[1,1,4096,512]{3,2,1,0:T(8,128)S(1)} %bitcast.1) | data formatting | bytes 16777216

commit v8 on v5

--- a/solution.py
+++ b/solution.py
@@ -274,10 +274,10 @@
         def _():
             leave_row(part, inner(i), near_send, i)
 
+        if i >= 2 * LAG:
+            land(i - 2 * LAG)
         if i >= LAG:
             change_plane(i - LAG)
-        if i >= 2 * LAG:
-            land(i - 2 * LAG)
         if i == 1:
 
             @pl.when(second == 1)

time: 192 us -> 192 us (level)
  no operation moved by 1% of the time
where the time goes in v8:
time: 192 us
  Pallas kernels  189 us (98%)
  local copies, waits for them, and re-layouts  3.4 us (2%)
    pallas_call x1, Pallas kernels, local(): pl.pallas_call(functools.partial(kernel, n, sizes), out_shape=buffer(step...  189 us

profile of v8, /device:TPU:1, one launch (start us, length us, event | category | flops | bytes accessed | tf_op | source)
XLA Modules:
  0.0 192.0 jit_solution(383126139575922503)
XLA Ops:
  0.0 188.6 %echo.1 = f32[4096,512]{1,0:T(8,128)S(1)} custom-call(f32[1,1,4096,512]{3,2,1,0:T(8,128)} %signal.1, f32[3,512]{1,0:T(4,128)} %gain.1), custom_call_target="tpu_custom_call" | custom-call | tf_op jit(solution)/shard_map/echo/pallas_call | solution.py:346
  188.6 3.4 %copy.4 = f32[1,1,4096,512]{3,2,1,0:T(8,128)} copy(f32[1,1,4096,512]{3,2,1,0:T(8,128)S(1)} %bitcast.1) | data formatting | bytes 16777216
